TPU v7x, 512 devices: a whole 4x8x8 slice. The times are simulated.
512 devices in a mesh: row: 16 (over x, y_lo, core), col: 32 (over z, y_hi).
Axes of the slice: x: 4, y: 8 (y_hi: 4, y_lo: 2; y = y_hi * 2 + y_lo), z: 8, core: 2. Of those that a mesh axis runs over, the one named last changes fastest.
Arguments:
- item_ids: int32 [131072], P(('row', 'col')), may hold values from 0 to 1023
- user_lengths: int32 [32], replicated, may hold values from 1 to 8192, 131072 in all
- catalogue: bfloat16 [1024, 1024], P(('row', 'col')), may hold values from -6 to 6
- tap_lengths: int32 [1, 1024], replicated, may hold values from 64 to 256
- conv_taps: bfloat16 [1, 256, 1024], replicated, may hold values from -0.375 to 0.375
- norm_gains: float32 [1, 2, 1024], replicated, may hold values from 0.1 to 1.9
- gate_weight: bfloat16 [1, 1024, 1024], P(None, 'col'), may hold values from -0.1875 to 0.1875
- up_weight: bfloat16 [1, 1024, 1024], P(None, 'col'), may hold values from -0.1875 to 0.1875
- down_weight: bfloat16 [1, 1024, 1024], P(None, 'col'), may hold values from -0.1875 to 0.1875
Outputs:
- history_out: bfloat16 [131072, 1024], P(('row', 'col'))
Inputs may be any that keep to these rules, and one draw needn't show every extreme that they name: `user_lengths`: the 32 lengths sum to 131072.
All inputs are finite; a program needn't handle non-finite values.
Results may differ from a plain program's by a relative error of at most 0.0054.
Values may be sent and summed in bfloat16 or wider, within the bound.
A program may use at most 64 MiB of HBM per device.

v0:
```python
import jax
import jax.numpy as jnp
from jax import lax
from jax.sharding import Mesh
from jax.sharding import PartitionSpec as P

ROW_COL = ("row", "col_0", "col_1")
COL = ("col_0", "col_1")
epsilon = 1e-06
group_taps = 32


def from_behind(block, axis, distance):
    devices = range(lax.axis_size(axis))
    route = [(i - distance, i) for i in devices if i - distance in devices]
    return lax.ppermute(block, axis, route)


def in_one_piece(arrays, axis, dim, along):
    both = jnp.concatenate(arrays, axis=along)
    result, at, outs = (lax.all_gather(both, axis, axis=dim, tiled=True), 0, [])
    for a in arrays:
        outs.append(lax.slice_in_dim(result, at, at + a.shape[along], axis=along))
        at += a.shape[along]
    return tuple(outs)


def whole_of(array, axes, dim):
    result = array
    for number in range(len(axes) - 1, -1, -1):
        result = lax.all_gather(result, axes[number], axis=dim, tiled=True)
    return result


def rms_norm(values, gains):
    scale = lax.rsqrt(jnp.mean(values * values, axis=-1, keepdims=True) + epsilon)
    return values * scale * gains


def token_ages(positions, user_starts):
    reached = user_starts[None, :] <= positions[:, None]
    fallback = jnp.minimum(positions, 0)[:, None]
    seg_start = jnp.max(jnp.where(reached, user_starts[None, :], fallback), axis=1)
    return positions - seg_start


def earlier_items(item_ids, wanted):
    current = item_ids
    pieces = []
    current = from_behind(current, ROW_COL, 1)
    pieces = [current] + pieces
    return pieces[0][-wanted:]


def convolve(extended, tap_table, token_age, out_rows):
    reach = extended.shape[0] - out_rows
    groups = -(-tap_table.shape[0] // group_taps)

    def one_group(group_index, accumulated):
        for within in range(group_taps):
            lag_index = group_index * group_taps + within
            shifted = lax.dynamic_slice_in_dim(extended, reach - lag_index, out_rows, 0)
            weights = lax.dynamic_slice_in_dim(tap_table, lag_index, 1, 0)
            keep = (lag_index <= token_age)[:, None]
            accumulated = accumulated + jnp.where(keep, shifted * weights, 0.0)
        return accumulated

    blank = jnp.zeros((out_rows, extended.shape[1]), jnp.float32)
    return lax.fori_loop(0, groups, one_group, blank)


def feed_forward(hidden, gains_row, gate_rows, up_rows, down_rows):
    inner = rms_norm(hidden, gains_row).astype(jnp.bfloat16)
    shards = in_one_piece((gate_rows, up_rows), COL, 0, 1)
    columns = inner
    first_sum = jnp.dot(columns, shards[0], preferred_element_type=jnp.float32)
    second_sum = jnp.dot(columns, shards[1], preferred_element_type=jnp.float32)
    activated = (jax.nn.silu(first_sum) * second_sum).astype(jnp.bfloat16)
    columns = activated
    projected = jnp.dot(columns, whole_of(down_rows, COL, 0), preferred_element_type=jnp.float32)
    return hidden + projected


def body(
    item_ids,
    user_lengths,
    catalogue,
    tap_lengths,
    conv_taps,
    norm_gains,
    gate_weight,
    up_weight,
    down_weight,
):
    row_count = item_ids.shape[0]
    reach = conv_taps.shape[1] - 1
    layer_count = conv_taps.shape[0]
    catalogue_all = lax.all_gather(catalogue, ROW_COL, axis=0, tiled=True)
    device_index = lax.axis_index("row") * lax.axis_size(COL) + lax.axis_index(COL)
    first_row = device_index * row_count
    user_starts = jnp.cumsum(user_lengths) - user_lengths
    lag_column = jnp.arange(conv_taps.shape[1], dtype=jnp.int32)[:, None]
    tap_tables = conv_taps.astype(jnp.float32) * (
        lag_column[None] < tap_lengths[:, None, :]
    ).astype(jnp.float32)
    extra = reach * layer_count
    wide_ids = jnp.concatenate([earlier_items(item_ids, extra), item_ids], axis=0)
    hidden = jnp.take(catalogue_all, wide_ids, axis=0).astype(jnp.float32)
    positions = first_row - extra + jnp.arange(row_count + extra, dtype=jnp.int32)
    all_ages = token_ages(positions, user_starts)
    out_rows = row_count + reach * (layer_count - 1)
    normed = rms_norm(hidden, norm_gains[0, 0]).astype(jnp.bfloat16)
    hidden = hidden[-out_rows:] + convolve(normed, tap_tables[0], all_ages[-out_rows:], out_rows)
    hidden = feed_forward(hidden, norm_gains[0, 1], gate_weight[0], up_weight[0], down_weight[0])
    return hidden.astype(jnp.bfloat16)


def solution(mesh):
    finer = Mesh(mesh.devices.reshape(mesh.shape["row"], 8, 4), ("row", "col_0", "col_1"))
    placed = (
        P(ROW_COL),
        P(),
        P(ROW_COL, None),
        P(),
        P(),
        P(),
        P(None, COL, None),
        P(None, COL, None),
        P(None, COL, None),
    )
    return jax.shard_map(
        body, mesh=finer, in_specs=placed, out_specs=P(ROW_COL, None), check_vma=False
    )
```

profile of v0, /device:TPU:2, one launch (start us, length us, event | category | flops | bytes accessed | tf_op | source)
XLA Modules:
  0.0 1239.3 jit_solution(7251413055012605955)
XLA Ops:
  6.5 0.0 all-gather.11.cloned.1.call-start
  6.5 0.7 all-gather.11.cloned.1.call-update
  7.3 0.0 all-gather.7.cloned.1.call-start
  7.3 1.5 pad_maximum_fusion
  8.8 0.0 all-gather.7.cloned.1.call-update
  8.9 0.0 all-gather.9.cloned.1.call-start
  8.9 4.5 collective-permute-start
  13.4 16.6 %all-gather = bf16[1,128,1024]{2,1,0:T(8,128)(2,1)} all-gather(bf16[1,32,1024]{2,1,0:T(8,128)(2,1)} %param.19), channel_id=2, replica_groups=mesh['row'=16,'col_0'=8,'col_1'=4] {'col_1'}, dimensions={1}, use_global_device_ids=true | all-gather | bytes 327680 | tf_op jit(solution)/shard_map/all_gather | solution.py:31
  30.0 0.0 all-gather.9.cloned.1.call-update
  30.1 0.7 copy.13
  30.8 0.1 reduce-window.9
  30.9 0.1 reduce
  31.0 0.7 sub.362
  31.6 0.8 fusion.52
  32.4 2.2 select_bitcast_fusion
  34.7 0.1 select_reduce_fusion
  34.8 0.1 slice.23
  34.9 0.0 collective-permute-done
  34.9 0.1 slice.21
  34.9 0.0 copy-done.3
  34.9 0.1 compare_and_fusion
  35.0 0.1 compare_select_fusion
  35.1 1044.8 %all-gather.11.cloned.1.call-done = bf16[512,2,1024]{2,1,0:T(2,128)(2,1)} async-done(((bf16[1,2,1024]{2,1,0:T(2,128)(2,1)}), bf16[512,2,1024]{2,1,0:T(2,128)(2,1)}) %all-gather.11.cloned.1.call-update) | async-done | bytes 2097168 | tf_op jit(solution)/shard_map/all_gather | solution.py:98
  1079.9 2.7 reshape.388
  1082.6 2.8 gather_fusion
  1085.4 1.7 multiply_reduce_fusion
  1087.1 1.6 multiply_convert_fusion
  1088.7 0.0 copy-start
  1088.7 125.7 %while.17 = (s32[]{:T(128)}, f32[256,1024]{1,0:T(8,128)S(1)}, s32[256]{0:T(256)S(1)}, bf16[511,1024]{1,0:T(8,128)(2,1)S(1)}, f32[256,1024]{1,0:T(8,128)}, /*inde...) while((s32[]{:T(128)}, f32[256,1024]{1,0:T(8,128)S(1)}, ...), condition=%wide.region_4.5_spmd.clone, body=%wide.region_3.4_spmd.clone.sunk | while | flops 33825024 | bytes 19289948 | solution.py:69
  1088.8 1.3 constant_dynamic-slice_fusion.35
  1090.2 1.4 constant_dynamic-slice_fusion.34
  1092.0 12.2 select_add_fusion.3
  1104.3 1.4 constant_dynamic-slice_fusion.35
  1105.9 1.5 constant_dynamic-slice_fusion.34
  1107.7 12.2 select_add_fusion.3
  1120.0 1.5 constant_dynamic-slice_fusion.35
  1121.6 1.4 constant_dynamic-slice_fusion.34
  1123.4 12.2 select_add_fusion.3
  1135.7 1.5 constant_dynamic-slice_fusion.35
  1137.3 1.4 constant_dynamic-slice_fusion.34
  1139.1 12.2 select_add_fusion.3
  1151.4 1.4 constant_dynamic-slice_fusion.35
  1152.9 1.7 constant_dynamic-slice_fusion.34
  1155.0 12.2 select_add_fusion.3
  1167.3 1.4 constant_dynamic-slice_fusion.35
  1168.8 1.7 constant_dynamic-slice_fusion.34
  1170.9 12.2 select_add_fusion.3
  1183.2 1.3 constant_dynamic-slice_fusion.35
  1184.6 1.7 constant_dynamic-slice_fusion.34
  1186.7 12.2 select_add_fusion.3
  1199.0 1.3 constant_dynamic-slice_fusion.35
  1200.4 1.4 constant_dynamic-slice_fusion.34
  1202.2 12.2 select_add_fusion.3
  1214.4 0.0 copy-done
  1214.4 0.2 fusion.51
  1214.6 0.0 copy-start.1
  1214.6 1.3 copy-done.1
  1216.0 0.3 multiply_reduce_fusion.1
  1216.2 0.0 all-gather.7.cloned.1.call-done
  1216.3 0.0 copy-start.2
  1216.3 3.9 fusion.26
  1220.2 7.7 all-gather.9.cloned.1.call-done
  1228.0 0.0 copy-done.2
  1228.0 4.8 fusion.39
  (23 shorter events, 0.6 us)
Async XLA Ops:
  6.5 28.4 %copy-start.3 = (s32[256]{0:T(256)S(1)}, s32[256]{0:T(256)}, u32[]{:S(2)}) copy-start(s32[256]{0:T(256)} %param.11) | copy-start | bytes 3076
  6.5 1073.3 %all-gather.11.cloned.1.call-start = ((), (), s32[]{:S(2)}) async-start(), calls=%async_computation.2 | async-start | bytes 2101248 | tf_op jit(solution)/shard_map/all_gather | solution.py:98
  7.3 1209.0 %all-gather.7.cloned.1.call-start = ((), (), s32[]{:S(2)}) async-start(), calls=%async_computation | async-start | bytes 4325376 | tf_op jit(solution)/shard_map/all_gather | solution.py:21
  8.9 1219.1 %all-gather.9.cloned.1.call-start = ((), (), s32[]{:S(2)}) async-start(), calls=%async_computation.1 | async-start | bytes 2359296 | tf_op jit(solution)/shard_map/all_gather | solution.py:31
  8.9 25.9 %collective-permute-start = (s32[256]{0:T(256)}, s32[256]{0:T(256)S(1)}, u32[]{:S(2)}, u32[]{:S(2)}) collective-permute-start(s32[256]{0:T(256)} %param.11), channel_id=1, source_target_pairs={{0,1},{1,2},{2,3},{3,4},{4,5},{5,6},{6,7},{7,8},{8,9},{9,10},{10,1... | collective-permute-start | bytes 3080 | tf_op jit(solution)/shard_map/ppermute | solution.py:16
  1088.7 125.7 %copy-start = (bf16[511,1024]{1,0:T(8,128)(2,1)S(1)}, bf16[511,1024]{1,0:T(8,128)(2,1)}, u32[]{:S(2)}) copy-start(bf16[511,1024]{1,0:T(8,128)(2,1)} %gather_fusion) | copy-start | bytes 3139588
  1214.6 1.3 copy-start.1
  1216.3 11.7 copy-start.2
Sparse Core Ops, SparseCore 0:
  9.5 1070.3 all-gather.10
  1083.0 103.2 all-gather.6
  1188.4 39.5 all-gather.8
where the time goes:
time: 1240 us
  waiting for transfers between devices  1050 us (85%)
  other arithmetic  107 us (9%)
  local copies, waits for them, and re-layouts  31.9 us (3%)
  blocking collectives  16.6 us (1%)
  between operations  13.2 us (1%)
    all_gather x1, waiting for transfers between devices, body(): catalogue_all = lax.all_gather(catalogue, ROW_COL, axis=0, tiled=True)  1040 us
    add x8, other arithmetic, one_group(): accumulated = accumulated + jnp.where(keep, shifted * weights, 0.0)  97.5 us
  transfers between devices with their start and end apart: 4, of which 2 were waited for; matrix products, arithmetic and copies ran while one was open for 11% of the time, Pallas kernels for 0%

commit v1 on v0

--- a/solution.py
+++ b/solution.py
@@ -95,7 +95,9 @@
     row_count = item_ids.shape[0]
     reach = conv_taps.shape[1] - 1
     layer_count = conv_taps.shape[0]
-    catalogue_all = lax.all_gather(catalogue, ROW_COL, axis=0, tiled=True)
+    catalogue_all = jnp.concatenate(
+        lax.all_to_all(jnp.stack([catalogue] * lax.axis_size(ROW_COL)), ROW_COL, 0, 0), axis=0
+    )
     device_index = lax.axis_index("row") * lax.axis_size(COL) + lax.axis_index(COL)
     first_row = device_index * row_count
     user_starts = jnp.cumsum(user_lengths) - user_lengths

time: 1240 us -> 248 us (0.20)
  the two profiles are of different devices: /device:TPU:2 before, /device:TPU:16 now
where the time goes in v1:
time: 248 us; the launch traced here: 246 us
  other arithmetic  105 us (42%)
  blocking collectives  52.1 us (21%)
  local copies, waits for them, and re-layouts  33.6 us (14%)
  starting transfers between devices  28.7 us (12%)
  between operations  13.6 us (5%)
  matrix products  8.71 us (4%)
  loops' own time  4.23 us (2%)
    add x8, other arithmetic, one_group(): accumulated = accumulated + jnp.where(keep, shifted * weights, 0.0)  97.5 us
    all_gather x1, blocking collectives, whole_of(): result = lax.all_gather(result, axes[number], axis=dim, tiled=True)  52.1 us
    dynamic_slice x16, local copies, waits for them, and re-layouts, one_group(): weights = lax.dynamic_slice_in_dim(tap_table, lag_index, 1, 0)  23.3 us
    all_to_all x1, starting transfers between devices, body(): lax.all_to_all(jnp.stack([catalogue] * lax.axis_size(ROW_COL)), ROW_COL,...  23.1 us
    ppermute x1, starting transfers between devices, from_behind(): return lax.ppermute(block, axis, route)  5.59 us
  transfers between devices with their start and end apart: 4, of which 0 were waited for; matrix products, arithmetic and copies ran while one was open for 57% of the time, Pallas kernels for 0%

profile of v1, /device:TPU:16, one launch (start us, length us, event | category | flops | bytes accessed | tf_op | source)
XLA Modules:
  0.0 246.0 jit_solution(17726425656835040291)
XLA Ops:
  6.5 0.0 all-gather.5.cloned.1.call-start
  6.5 1.5 pad_maximum_fusion
  8.1 0.0 all-gather.5.cloned.1.call-update
  8.1 3.1 %stack.2 = bf16[512,2,1024]{2,1,0:T(2,128)(2,1)} broadcast(bf16[2,1024]{1,0:T(2,128)(2,1)} %param.13), dimensions={1,2} | broadcast | bytes 2101248 | tf_op jit(solution)/shard_map/stack | solution.py:99
  11.2 0.0 copy-start.3
  11.2 0.0 copy-start.6
  11.3 23.1 %all-to-all-start = ((bf16[512,2,1024]{2,1,0:T(2,128)(2,1)}), bf16[512,2,1024]{2,1,0:T(2,128)(2,1)}, u32[]{:S(2)}, u32[]{:S(2)}) async-start(bf16[512,2,1024]{2,1,0:T(2,128)(2,1)} %stack.2), calls=%async_computation | async-start | bytes 4194304 | tf_op jit(solution)/shard_map/all_to_all | solution.py:99
  34.4 0.0 all-gather.7.cloned.1.call-start
  34.4 0.0 copy-done.7
  34.4 5.6 %collective-permute-start = (s32[256]{0:T(256)S(1)}, s32[256]{0:T(256)S(1)}, u32[]{:S(2)}, u32[]{:S(2)}) collective-permute-start(s32[256]{0:T(256)S(1)} %copy-done.7), channel_id=1, source_target_pairs={{0,1},{1,2},{2,3},{3,4},{4,5},{5,6},{6,7},{7,8},{8,9},{9,10},{10,1... | collective-permute-start | bytes 3080 | tf_op jit(solution)/shard_map/ppermute | solution.py:16
  40.0 0.0 copy-done.4
  40.0 52.1 %all-gather = bf16[1,128,1024]{2,1,0:T(8,128)(2,1)} all-gather(bf16[1,32,1024]{2,1,0:T(8,128)(2,1)S(1)} %copy-done.4), channel_id=2, replica_groups=mesh['row'=16,'col_0'=8,'col_1'=4] {'col_1'}, dimensions={1}, use_global_device_ids=true | all-gather | bytes 327680 | tf_op jit(solution)/shard_map/all_gather | solution.py:31
  92.2 0.0 all-gather.7.cloned.1.call-update
  92.2 0.0 copy-done.8
  92.2 0.1 copy.12
  92.3 0.1 reduce-window.9
  92.4 0.1 reduce
  92.5 0.1 select_reduce_fusion
  92.6 0.0 copy-done.5
  92.6 0.0 copy-done.3
  92.6 0.0 copy-done.6
  92.6 1.1 select_bitcast_fusion
  93.8 0.1 slice.23
  93.9 0.0 collective-permute-done
  93.9 0.1 slice.21
  93.9 0.1 compare_and_fusion
  94.0 0.1 compare_select_fusion
  94.1 0.0 all-to-all-done
  94.1 2.8 %reshape.380 = bf16[1024,1024]{1,0:T(8,128)(2,1)S(1)} reshape(bf16[512,2,1024]{2,1,0:T(2,128)(2,1)} %all-to-all-done) | data formatting | bytes 4194304 | tf_op jit(solution)/shard_map/reshape | solution.py:98
  96.9 2.8 %gather_fusion = bf16[511,1024]{1,0:T(8,128)(2,1)} fusion(bf16[1024,1024]{1,0:T(8,128)(2,1)S(1)} %reshape.380, s32[1024]{0:T(1024)S(1)} %pad_clamp_fusion), kind=kCustom, calls=%fused_computation | custom fusion | bytes 2095100 | tf_op jit(solution)/shard_map/jit(_take)/gather | solution.py:110
  99.7 1.7 multiply_reduce_fusion
  101.3 1.6 multiply_convert_fusion
  103.0 125.6 %while.17 = (s32[]{:T(128)}, f32[256,1024]{1,0:T(8,128)S(1)}, s32[256]{0:T(256)S(1)}, bf16[511,1024]{1,0:T(8,128)(2,1)S(1)}, f32[256,1024]{1,0:T(8,128)}, /*inde...) while((s32[]{:T(128)}, f32[256,1024]{1,0:T(8,128)S(1)}, ...), condition=%wide.region_4.5_spmd.clone, body=%wide.region_3.4_spmd.clone.sunk | while | flops 33825024 | bytes 19289948 | solution.py:69
  103.1 1.5 constant_dynamic-slice_fusion.35
  104.7 1.6 constant_dynamic-slice_fusion.34
  106.7 12.2 %select_add_fusion.3 = f32[256,1024]{1,0:T(8,128)S(1)} fusion(f32[256,1024]{1,0:T(8,128)S(1)} %get-tuple-element.605, f32[1024]{0:T(1024)S(1)} %bitcast.115, bf16[511,1024]{1,0:T(8,128)(2,1)S(1)} %get-tuple-element.679, s32[]{:T(128)S(6)} %select_n.1373, f32[1024]{0:T(1024)S(1)} %bitcast.116, s32[]{:T(128)S(6)} %select_n.1374, ...), kind=kLoop, calls=%fused_computation.26.clone.1 | loop fusion | flops 33816576 | bytes 19013760 | tf_op jit(solution)/shard_map/while/body/eval_jaxpr/add | solution.py:65
  119.0 1.5 constant_dynamic-slice_fusion.35
  120.6 1.5 constant_dynamic-slice_fusion.34
  122.4 12.2 %select_add_fusion.3 = f32[256,1024]{1,0:T(8,128)S(1)} fusion(f32[256,1024]{1,0:T(8,128)S(1)} %get-tuple-element.605, f32[1024]{0:T(1024)S(1)} %bitcast.115, bf16[511,1024]{1,0:T(8,128)(2,1)S(1)} %get-tuple-element.679, s32[]{:T(128)S(6)} %select_n.1373, f32[1024]{0:T(1024)S(1)} %bitcast.116, s32[]{:T(128)S(6)} %select_n.1374, ...), kind=kLoop, calls=%fused_computation.26.clone.1 | loop fusion | flops 33816576 | bytes 19013760 | tf_op jit(solution)/shard_map/while/body/eval_jaxpr/add | solution.py:65
  134.7 1.5 constant_dynamic-slice_fusion.35
  136.3 1.5 constant_dynamic-slice_fusion.34
  138.1 12.2 %select_add_fusion.3 = f32[256,1024]{1,0:T(8,128)S(1)} fusion(f32[256,1024]{1,0:T(8,128)S(1)} %get-tuple-element.605, f32[1024]{0:T(1024)S(1)} %bitcast.115, bf16[511,1024]{1,0:T(8,128)(2,1)S(1)} %get-tuple-element.679, s32[]{:T(128)S(6)} %select_n.1373, f32[1024]{0:T(1024)S(1)} %bitcast.116, s32[]{:T(128)S(6)} %select_n.1374, ...), kind=kLoop, calls=%fused_computation.26.clone.1 | loop fusion | flops 33816576 | bytes 19013760 | tf_op jit(solution)/shard_map/while/body/eval_jaxpr/add | solution.py:65
  150.4 1.5 constant_dynamic-slice_fusion.35
  152.0 1.4 constant_dynamic-slice_fusion.34
  153.8 12.2 %select_add_fusion.3 = f32[256,1024]{1,0:T(8,128)S(1)} fusion(f32[256,1024]{1,0:T(8,128)S(1)} %get-tuple-element.605, f32[1024]{0:T(1024)S(1)} %bitcast.115, bf16[511,1024]{1,0:T(8,128)(2,1)S(1)} %get-tuple-element.679, s32[]{:T(128)S(6)} %select_n.1373, f32[1024]{0:T(1024)S(1)} %bitcast.116, s32[]{:T(128)S(6)} %select_n.1374, ...), kind=kLoop, calls=%fused_computation.26.clone.1 | loop fusion | flops 33816576 | bytes 19013760 | tf_op jit(solution)/shard_map/while/body/eval_jaxpr/add | solution.py:65
  166.1 1.3 constant_dynamic-slice_fusion.35
  167.5 1.6 constant_dynamic-slice_fusion.34
  169.5 12.2 %select_add_fusion.3 = f32[256,1024]{1,0:T(8,128)S(1)} fusion(f32[256,1024]{1,0:T(8,128)S(1)} %get-tuple-element.605, f32[1024]{0:T(1024)S(1)} %bitcast.115, bf16[511,1024]{1,0:T(8,128)(2,1)S(1)} %get-tuple-element.679, s32[]{:T(128)S(6)} %select_n.1373, f32[1024]{0:T(1024)S(1)} %bitcast.116, s32[]{:T(128)S(6)} %select_n.1374, ...), kind=kLoop, calls=%fused_computation.26.clone.1 | loop fusion | flops 33816576 | bytes 19013760 | tf_op jit(solution)/shard_map/while/body/eval_jaxpr/add | solution.py:65
  181.8 1.2 constant_dynamic-slice_fusion.35
  183.1 1.5 constant_dynamic-slice_fusion.34
  185.0 12.2 %select_add_fusion.3 = f32[256,1024]{1,0:T(8,128)S(1)} fusion(f32[256,1024]{1,0:T(8,128)S(1)} %get-tuple-element.605, f32[1024]{0:T(1024)S(1)} %bitcast.115, bf16[511,1024]{1,0:T(8,128)(2,1)S(1)} %get-tuple-element.679, s32[]{:T(128)S(6)} %select_n.1373, f32[1024]{0:T(1024)S(1)} %bitcast.116, s32[]{:T(128)S(6)} %select_n.1374, ...), kind=kLoop, calls=%fused_computation.26.clone.1 | loop fusion | flops 33816576 | bytes 19013760 | tf_op jit(solution)/shard_map/while/body/eval_jaxpr/add | solution.py:65
  197.3 1.3 constant_dynamic-slice_fusion.35
  198.7 1.5 constant_dynamic-slice_fusion.34
  200.5 12.2 %select_add_fusion.3 = f32[256,1024]{1,0:T(8,128)S(1)} fusion(f32[256,1024]{1,0:T(8,128)S(1)} %get-tuple-element.605, f32[1024]{0:T(1024)S(1)} %bitcast.115, bf16[511,1024]{1,0:T(8,128)(2,1)S(1)} %get-tuple-element.679, s32[]{:T(128)S(6)} %select_n.1373, f32[1024]{0:T(1024)S(1)} %bitcast.116, s32[]{:T(128)S(6)} %select_n.1374, ...), kind=kLoop, calls=%fused_computation.26.clone.1 | loop fusion | flops 33816576 | bytes 19013760 | tf_op jit(solution)/shard_map/while/body/eval_jaxpr/add | solution.py:65
  212.8 1.5 constant_dynamic-slice_fusion.35
  214.4 1.6 constant_dynamic-slice_fusion.34
  216.4 12.2 %select_add_fusion.3 = f32[256,1024]{1,0:T(8,128)S(1)} fusion(f32[256,1024]{1,0:T(8,128)S(1)} %get-tuple-element.605, f32[1024]{0:T(1024)S(1)} %bitcast.115, bf16[511,1024]{1,0:T(8,128)(2,1)S(1)} %get-tuple-element.679, s32[]{:T(128)S(6)} %select_n.1373, f32[1024]{0:T(1024)S(1)} %bitcast.116, s32[]{:T(128)S(6)} %select_n.1374, ...), kind=kLoop, calls=%fused_computation.26.clone.1 | loop fusion | flops 33816576 | bytes 19013760 | tf_op jit(solution)/shard_map/while/body/eval_jaxpr/add | solution.py:65
  228.6 0.2 fusion.51
  228.8 0.0 copy-start.1
  228.8 1.3 copy-done.1
  230.2 0.3 multiply_reduce_fusion.1
  230.4 0.0 all-gather.5.cloned.1.call-done
  230.5 3.9 %fusion.26 = f32[256,1024]{1,0:T(8,128)} fusion(bf16[1024,2048]{1,0:T(8,128)(2,1)} %all-gather.5.cloned.1.call-done, f32[1024]{0:T(1024)S(1)} %bitcast.153, f32[256]{0:T(256)S(1)} %add_rsqrt_fusion.1, f32[256,1024]{1,0:T(8,128)S(1)} %get-tuple-element.276, f32[511,1024]{1,0:T(8,128)} %copy-done.1), kind=kOutput, calls=%fused_computation.93 | convolution fusion | flops 537919488 | bytes 5248000 | tf_op jit(solution)/shard_map/dot_general | solution.py:76
  234.4 4.8 %fusion.39 = bf16[256,1024]{1,0:T(8,128)(2,1)} fusion(bf16[1,1024,1024]{2,1,0:T(8,128)(2,1)} %all-gather.7.cloned.1.call-done, bf16[1024,2048]{1,0:T(8,128)(2,1)} %all-gather.5.cloned.1.call-done, f32[256,1024]{1,0:T(8,128)} %fusion.26, f32[1024]{0:T(1024)S(1)} %bitcast.154, f32[256]{0:T(256)S(1)} %add_rsqrt_fusion.1, ...), kind=kOutput, calls=%fused_computation.102 | convolution fusion | flops 1077149696 | bytes 9966592 | tf_op jit(solution)/shard_map/dot_general | solution.py:80
  (33 shorter events, 0.6 us)
Async XLA Ops:
  6.5 223.9 %all-gather.5.cloned.1.call-start = ((), (), s32[]{:S(2)}) async-start(), calls=%async_computation.1 | async-start | bytes 4325376 | tf_op jit(solution)/shard_map/all_gather | solution.py:21
  11.2 23.2 %copy-start.7 = (s32[256]{0:T(256)S(1)}, s32[256]{0:T(256)}, u32[]{:S(2)}) copy-start(s32[256]{0:T(256)} %param.11) | copy-start | bytes 3076
  11.2 28.8 %copy-start.4 = (bf16[1,32,1024]{2,1,0:T(8,128)(2,1)S(1)}, bf16[1,32,1024]{2,1,0:T(8,128)(2,1)}, u32[]{:S(2)}) copy-start(bf16[1,32,1024]{2,1,0:T(8,128)(2,1)} %param.19) | copy-start | bytes 196612
  11.2 81.0 %copy-start.8 = (s32[32]{0:T(128)S(1)}, s32[32]{0:T(128)}, u32[]{:S(2)}) copy-start(s32[32]{0:T(128)} %param.12) | copy-start | bytes 388
  11.2 81.4 %copy-start.5 = (f32[1,2,1024]{2,1,0:T(2,128)S(1)}, f32[1,2,1024]{2,1,0:T(2,128)}, u32[]{:S(2)}) copy-start(f32[1,2,1024]{2,1,0:T(2,128)} %param.16) | copy-start | bytes 24580
  11.2 81.4 %copy-start.3 = (bf16[1,256,1024]{2,1,0:T(8,128)(2,1)S(1)}, bf16[1,256,1024]{2,1,0:T(8,128)(2,1)}, u32[]{:S(2)}) copy-start(bf16[1,256,1024]{2,1,0:T(8,128)(2,1)} %param.15) | copy-start | bytes 1572868
  11.2 81.4 %copy-start.6 = (s32[1,1024]{1,0:T(1,128)S(1)}, s32[1,1024]{1,0:T(1,128)}, u32[]{:S(2)}) copy-start(s32[1,1024]{1,0:T(1,128)} %param.14) | copy-start | bytes 12292
  11.3 82.8 %all-to-all-start = ((bf16[512,2,1024]{2,1,0:T(2,128)(2,1)}), bf16[512,2,1024]{2,1,0:T(2,128)(2,1)}, u32[]{:S(2)}, u32[]{:S(2)}) async-start(bf16[512,2,1024]{2,1,0:T(2,128)(2,1)} %stack.2), calls=%async_computation | async-start | bytes 4194304 | tf_op jit(solution)/shard_map/all_to_all | solution.py:99
  34.4 200.1 %all-gather.7.cloned.1.call-start = ((), (), s32[]{:S(2)}) async-start(), calls=%async_computation.2 | async-start | bytes 2359296 | tf_op jit(solution)/shard_map/all_gather | solution.py:31
  34.4 59.5 %collective-permute-start = (s32[256]{0:T(256)S(1)}, s32[256]{0:T(256)S(1)}, u32[]{:S(2)}, u32[]{:S(2)}) collective-permute-start(s32[256]{0:T(256)S(1)} %copy-done.7), channel_id=1, source_target_pairs={{0,1},{1,2},{2,3},{3,4},{4,5},{5,6},{6,7},{7,8},{8,9},{9,10},{10,1... | collective-permute-start | bytes 3080 | tf_op jit(solution)/shard_map/ppermute | solution.py:16
  102.9 125.7 %copy-start = (bf16[511,1024]{1,0:T(8,128)(2,1)S(1)}, bf16[511,1024]{1,0:T(8,128)(2,1)}, u32[]{:S(2)}) copy-start(bf16[511,1024]{1,0:T(8,128)(2,1)} %gather_fusion) | copy-start | bytes 3139588
  228.8 1.3 copy-start.1
  230.5 3.9 %copy-start.2 = (f32[511,1024]{1,0:T(8,128)S(1)}, f32[511,1024]{1,0:T(8,128)}, u32[]{:S(2)}) copy-start(f32[511,1024]{1,0:T(8,128)} %copy-done.1) | copy-start | bytes 6279172
Sparse Core Ops, SparseCore 0:
  10.5 134.5 all-gather.4
  147.2 41.5 all-gather.6
